TPU v7x, 32 devices: a whole 2x2x4 slice. The times are simulated.
32 devices in a mesh: etp: 4 (over z), ep: 8 (over y, x, core).
Axes of the slice: x: 2, y: 2, z: 4, core: 2. Of those that a mesh axis runs over, the one named last changes fastest.
Arguments:
- x_norm: bfloat16 [8192, 1536], P('ep')
- expert_ids: int32 [8192, 6], P('ep')
- sel_scores: float32 [8192, 6], P('ep')
- w_gate: bfloat16 [64, 1536, 512], P('ep', None, 'etp')
- w_up: bfloat16 [64, 1536, 512], P('ep', None, 'etp')
- w_down: bfloat16 [64, 512, 1536], P('ep', 'etp')
- ws_gate: bfloat16 [1536, 1024], P(None, 'etp')
- ws_up: bfloat16 [1536, 1024], P(None, 'etp')
- ws_down: bfloat16 [1024, 1536], P('etp')
- d_out: bfloat16 [8192, 1536], P('ep')
Outputs:
- output 1: bfloat16 [8192, 1536], P('ep')
- output 2: float32 [8192, 1536], P('ep')
- output 3: float32 [8192, 6], P('ep')
- output 4: float32 [64, 1536, 512], P('ep', None, 'etp')
- output 5: float32 [64, 1536, 512], P('ep', None, 'etp')
- output 6: float32 [64, 512, 1536], P('ep', 'etp')
- output 7: float32 [1536, 1024], P(None, 'etp')
- output 8: float32 [1536, 1024], P(None, 'etp')
- output 9: float32 [1024, 1536], P('etp')
All inputs are finite; a program needn't handle non-finite values.
Results may differ from a plain program's by a relative error of at most 0.0120727.
Values are sent between devices in bfloat16 or wider.
A program may use at most 1 GiB of HBM per device.

v0:
```python
import jax
import jax.numpy as jnp
from jax import lax
from jax.sharding import PartitionSpec as P

ROUTE_SCALE = 2.5


def gate_weights(scores):
    return ROUTE_SCALE * scores / jnp.sum(scores, axis=-1, keepdims=True)


def silu_parts(pre_act):
    logistic = jax.nn.sigmoid(pre_act)
    return pre_act * logistic, logistic * (1.0 + pre_act * (1.0 - logistic))


def slot_plan(shard_ids, num_experts, capacity):
    tok_count, top_k = shard_ids.shape
    flat_ids = shard_ids.reshape(-1)
    sort_order = jnp.argsort(flat_ids, stable=True)
    counts = jnp.bincount(flat_ids, length=num_experts)
    starts = jnp.cumsum(counts) - counts
    col_index = jnp.arange(capacity)
    slot_valid = col_index[None, :] < counts[:, None]
    slot_entry = sort_order[jnp.minimum(starts[:, None] + col_index[None, :], tok_count * top_k - 1)]
    entry_rank = jnp.argsort(sort_order) - starts[flat_ids]
    entry_slot = (flat_ids * capacity + entry_rank).reshape(tok_count, top_k)
    return slot_entry, slot_valid, entry_slot


def solution(mesh):
    ep_size = mesh.shape['ep']
    row_spec = P('ep', None)
    col_spec = P('ep', None, 'etp')
    down_spec = P('ep', 'etp', None)
    in_specs = (row_spec, row_spec, row_spec, col_spec, col_spec, down_spec, P(None, 'etp'), P(None, 'etp'), P('etp', None), row_spec)
    out_specs = (row_spec, row_spec, row_spec, col_spec, col_spec, down_spec, P(None, 'etp'), P(None, 'etp'), P('etp', None))

    def device_step(x_local, ids_local, scores_local, wg_local, wu_local, wd_local, sg_local, su_local, sd_local, dy_local):
        tok_count, top_k = ids_local.shape
        local_experts = wg_local.shape[0]
        num_experts = local_experts * ep_size
        hidden_dim = x_local.shape[1]
        capacity = 2 * tok_count * top_k // num_experts - 1
        buffer_shape = (ep_size, local_experts, capacity, hidden_dim)
        slot_entry, slot_valid, entry_slot = slot_plan(ids_local, num_experts, capacity)
        slot_token = slot_entry // top_k
        gates = gate_weights(scores_local)
        slot_gate = jnp.where(slot_valid, gates.reshape(-1)[slot_entry], 0.0)

        x_send = jnp.where(slot_valid[:, :, None], x_local[slot_token], jnp.zeros((), x_local.dtype))
        x_recv = lax.all_to_all(x_send, 'ep', 0, 0, tiled=True).reshape(buffer_shape)
        gate_act = jnp.einsum('secd,edf->secf', x_recv, wg_local, preferred_element_type=jnp.float32)
        up_lin = jnp.einsum('secd,edf->secf', x_recv, wu_local, preferred_element_type=jnp.float32)
        silu_val, silu_grad = silu_parts(gate_act)
        hidden = (silu_val * up_lin).astype(jnp.bfloat16)
        part_out = jnp.einsum('secf,efd->secd', hidden, wd_local, preferred_element_type=jnp.float32).astype(jnp.bfloat16)
        out_back = lax.all_to_all(part_out.reshape(num_experts, capacity, hidden_dim), 'ep', 0, 0, tiled=True)
        out_rows = out_back.reshape(num_experts * capacity, hidden_dim)[entry_slot]
        routed = jnp.sum(out_rows * gates[:, :, None], axis=1)

        shared_act = jnp.dot(x_local, sg_local, preferred_element_type=jnp.float32)
        shared_lin = jnp.dot(x_local, su_local, preferred_element_type=jnp.float32)
        shared_val, shared_grad = silu_parts(shared_act)
        shared_hid = (shared_val * shared_lin).astype(jnp.bfloat16)
        shared_out = jnp.dot(shared_hid, sd_local, preferred_element_type=jnp.float32)
        y_out = lax.psum(routed + shared_out, 'etp').astype(jnp.bfloat16)

        gate_grad = lax.psum(jnp.einsum('td,tkd->tk', dy_local, out_rows, preferred_element_type=jnp.float32), 'etp')
        _, gate_pull = jax.vjp(gate_weights, scores_local)
        d_scores = gate_pull(gate_grad)[0]

        dy_send = (slot_gate[:, :, None] * dy_local[slot_token]).astype(jnp.bfloat16)
        dy_recv = lax.all_to_all(dy_send, 'ep', 0, 0, tiled=True).reshape(buffer_shape)
        d_hidden = jnp.einsum('secd,efd->secf', dy_recv, wd_local, preferred_element_type=jnp.float32)
        dw_down = jnp.einsum('secf,secd->efd', hidden, dy_recv, preferred_element_type=jnp.float32)
        d_act = (d_hidden * up_lin * silu_grad).astype(jnp.bfloat16)
        d_lin = (d_hidden * silu_val).astype(jnp.bfloat16)
        dw_gate = jnp.einsum('secd,secf->edf', x_recv, d_act, preferred_element_type=jnp.float32)
        dw_up = jnp.einsum('secd,secf->edf', x_recv, d_lin, preferred_element_type=jnp.float32)
        dx_part = jnp.einsum('secf,edf->secd', d_act, wg_local, preferred_element_type=jnp.float32) + jnp.einsum('secf,edf->secd', d_lin, wu_local, preferred_element_type=jnp.float32)
        dx_back = lax.all_to_all(dx_part.astype(jnp.bfloat16).reshape(num_experts, capacity, hidden_dim), 'ep', 0, 0, tiled=True)
        dx_routed = jnp.sum(dx_back.reshape(num_experts * capacity, hidden_dim)[entry_slot], axis=1, dtype=jnp.float32)

        shared_dh = jnp.einsum('td,fd->tf', dy_local, sd_local, preferred_element_type=jnp.float32)
        shared_da = (shared_dh * shared_lin * shared_grad).astype(jnp.bfloat16)
        shared_db = (shared_dh * shared_val).astype(jnp.bfloat16)
        dws_down = lax.psum(jnp.einsum('tf,td->fd', shared_hid, dy_local, preferred_element_type=jnp.float32), 'ep')
        dws_gate = lax.psum(jnp.einsum('td,tf->df', x_local, shared_da, preferred_element_type=jnp.float32), 'ep')
        dws_up = lax.psum(jnp.einsum('td,tf->df', x_local, shared_db, preferred_element_type=jnp.float32), 'ep')
        dx_shared = jnp.einsum('tf,df->td', shared_da, sg_local, preferred_element_type=jnp.float32) + jnp.einsum('tf,df->td', shared_db, su_local, preferred_element_type=jnp.float32)
        dx_norm = lax.psum(dx_routed + dx_shared, 'etp')
        return (y_out, dx_norm, d_scores, dw_gate, dw_up, dw_down, dws_gate, dws_up, dws_down)

    return jax.shard_map(device_step, mesh=mesh, in_specs=in_specs, out_specs=out_specs, check_vma=False)
```

profile of v0, /device:TPU:0, one launch (start us, length us, event | category | flops | bytes accessed | tf_op | source)
XLA Modules:
  0.0 3087.9 jit_solution(2126833029195529156)
XLA Ops:
  12.8 42.9 %scatter_custom_fusion = s32[64]{0:T(128)S(1)} fusion(s32[6144]{0:T(1024)S(1)} %bitcast.199, s32[6144]{0:T(1024)S(1)} %broadcast.353, s32[]{:T(128)} %constant.14.clone.1), kind=kCustom, calls=%fused_computation.148 | custom fusion | flops 6144 | bytes 260 | tf_op jit(solution)/shard_map/scatter-add | solution.py:22
  63.8 67.7 %gather_fusion = s32[12224]{0:T(1024)S(1)} fusion(s32[6144]{0:T(1024)S(1)} %get-tuple-element.11, s32[12288]{0:T(1024)S(1)} %pad_clamp_fusion.2), kind=kCustom, calls=%fused_computation | custom fusion | bytes 146688 | tf_op jit(solution)/shard_map/gather | solution.py:26
  132.6 75.7 %gather_fusion.1 = bf16[12224,1536]{1,0:T(8,128)(2,1)} fusion(bf16[1024,1536]{1,0:T(8,128)(2,1)} %param.10, s32[12288]{0:T(1024)S(1)} %pad_clamp_fusion.1), kind=kCustom, calls=%fused_computation.1 | custom fusion | bytes 75153152 | tf_op jit(solution)/shard_map/gather | solution.py:52
  208.3 46.9 %reshape.306 = bf16[64,191,1536]{2,1,0:T(8,128)(2,1)} reshape(bf16[12224,1536]{1,0:T(8,128)(2,1)} %gather_fusion.1) | data formatting | bytes 75104256 | tf_op jit(solution)/shard_map/gather | solution.py:52
  255.3 25.9 broadcast_select_fusion
  292.3 67.7 %gather_fusion.3 = f32[12224]{0:T(1024)S(1)} fusion(f32[6144]{0:T(1024)S(1)} %reshape.293, s32[12288]{0:T(1024)S(1)} %pad_clamp_fusion), kind=kCustom, calls=%fused_computation.3 | custom fusion | bytes 146688 | tf_op jit(solution)/shard_map/gather | solution.py:50
  360.3 75.7 %gather_fusion.4 = bf16[12224,1536]{1,0:T(8,128)(2,1)} fusion(bf16[1024,1536]{1,0:T(8,128)(2,1)} %param.19, s32[12288]{0:T(1024)S(1)} %pad_clamp_fusion.1), kind=kCustom, calls=%fused_computation.4 | custom fusion | bytes 75153152 | tf_op jit(solution)/shard_map/gather | solution.py:74
  436.0 56.6 %reshape.431 = f32[64,191,1536]{2,1,0:T(8,128)} reshape(bf16[12224,1536]{1,0:T(8,128)(2,1)} %gather_fusion.4) | data formatting | bytes 112656384 | tf_op jit(solution)/shard_map/convert_element_type | solution.py:74
  492.7 37.1 %multiply_convert_fusion = bf16[64,191,1536]{2,1,0:T(8,128)(2,1)} fusion(f32[64,191,1536]{2,1,0:T(8,128)} %reshape.431, f32[64,191]{1,0:T(8,128)S(1)} %broadcast_select_fusion.1), kind=kLoop, calls=%fused_computation.8 | loop fusion | flops 37552128 | bytes 112705280 | tf_op jit(solution)/shard_map/convert_element_type | solution.py:74
  529.8 168.8 %all-to-all-done = bf16[64,191,1536]{2,1,0:T(8,128)(2,1)} async-done(((bf16[64,191,1536]{2,1,0:T(8,128)(2,1)}), bf16[64,191,1536]{2,1,0:T(8,128)(2,1)}, u32[]{:S(2)}, u32[]{:S(2)}) %all-to-all-start) | async-done | bytes 37552160 | tf_op jit(solution)/shard_map/all_to_all | solution.py:53
  744.9 370.0 %all-to-all-done.2 = bf16[64,191,1536]{2,1,0:T(8,128)(2,1)} async-done(((bf16[64,191,1536]{2,1,0:T(8,128)(2,1)}), bf16[64,191,1536]{2,1,0:T(8,128)(2,1)}, u32[]{:S(2)}, u32[]{:S(2)}) %all-to-all-start.2) | async-done | bytes 37552160 | tf_op jit(solution)/shard_map/all_to_all | solution.py:75
  1114.9 22.3 fusion.15
  1155.4 34.9 %copy.100 = bf16[8,8,191,1536]{3,1,0,2:T(8,128)(2,1)} copy(bf16[8,8,191,1536]{3,2,0,1:T(8,128)(2,1)} %convert_bitcast_fusion) | data formatting | bytes 75104256 | tf_op jit(solution)/shard_map/convert_element_type | solution.py:58
  1190.3 43.7 %copy.49 = bf16[64,191,1536]{2,1,0:T(8,128)(2,1)} copy(bf16[64,191,1536]{2,0,1:T(8,128)(2,1)} %bitcast.195) | data formatting | bytes 75104256 | tf_op jit(solution)/shard_map/reshape | solution.py:59
  1241.8 28.9 fusion.35
  1270.7 40.3 %fusion = bf16[8,8,191,1536]{3,2,0,1:T(8,128)(2,1)} fusion(f32[8,8,191,1536]{3,2,1,0:T(8,128)} %fusion.35, bf16[8,8,191,128]{3,2,0,1:T(8,128)(2,1)} %get-tuple-element.104, bf16[8,1536,128]{2,1,0:T(8,128)(2,1)} %param.14), kind=kOutput, calls=%fused_computation.10 | convolution fusion | flops 4844224512 | bytes 118931456 | tf_op jit(solution)/shard_map/secf,edf->secd/dot_general | solution.py:82
  1311.0 34.9 %copy.99 = bf16[8,8,191,1536]{3,1,0,2:T(8,128)(2,1)} copy(bf16[8,8,191,1536]{3,2,0,1:T(8,128)(2,1)} %fusion) | data formatting | bytes 75104256 | tf_op jit(solution)/shard_map/convert_element_type | solution.py:83
  1345.9 35.0 %copy.55 = bf16[64,191,1536]{2,1,0:T(8,128)(2,1)} copy(bf16[64,191,1536]{2,0,1:T(8,128)(2,1)} %bitcast.196) | data formatting | bytes 75104256 | tf_op jit(solution)/shard_map/reshape | solution.py:83
  1380.9 269.7 %all-to-all-done.1 = bf16[64,191,1536]{2,1,0:T(8,128)(2,1)} async-done(((bf16[64,191,1536]{2,1,0:T(8,128)(2,1)}), bf16[64,191,1536]{2,1,0:T(8,128)(2,1)}, u32[]{:S(2)}, u32[]{:S(2)}) %all-to-all-start.1) | async-done | bytes 37552160 | tf_op jit(solution)/shard_map/all_to_all | solution.py:59
  1688.2 36.1 %fusion.42 = s32[6144]{0:T(1024)S(1)} fusion(s32[6144]{0:T(1024)S(1)} %get-tuple-element.12, pred[6144]{0:T(1024)(128)(4,1)S(1)} %get-tuple-element.96, pred[6144]{0:T(1024)(128)(4,1)S(1)} %get-tuple-element.95, pred[6144]{0:T(1024)(128)(4,1)S(1)} %get-tuple-element.94, pred[6144]{0:T(1024)(128)(4,1)S(1)} %get-tuple-element.93, ...), kind=kLoop, calls=%fused_computation.144 | loop fusion | flops 368640 | bytes 448740 | tf_op jit(solution)/shard_map/add | solution.py:28
  1729.5 322.9 %all-reduce.8.cloned.1.call-done = (f32[1536,256]{0,1:T(8,128)}, f32[1536,256]{0,1:T(8,128)}, f32[256,1536]{1,0:T(8,128)}) async-done(((f32[1536,256]{0,1:T(8,128)}, f32[1536,256]{0,1:T(8,128)}, f32[256,1536]{1,0:T(8,128)}), (f32[1536,256]{0,1:T(8,128)}, f32[1536,256]{0,1:T(8,128)}, f32[256,1536]{1,0:T(8,128)})) %all-reduce.8.cloned.1.call-update) | async-done | bytes 4718608 | tf_op jit(solution)/shard_map/psum | solution.py:90
  2075.4 20.9 fusion.27
  2096.3 20.0 fusion.24
  2116.3 47.0 %reshape.291 = bf16[12224,1536]{1,0:T(8,128)(2,1)} reshape(bf16[64,191,1536]{2,1,0:T(8,128)(2,1)} %all-to-all-done.1) | data formatting | bytes 75104256 | tf_op jit(solution)/shard_map/reshape | solution.py:60
  2163.3 131.5 %gather_fusion.2 = bf16[6144,1536]{1,0:T(8,128)(2,1)} fusion(bf16[12224,1536]{1,0:T(8,128)(2,1)} %reshape.291, s32[6144]{0:T(1024)S(1)} %broadcast_clamp_fusion), kind=kCustom, calls=%fused_computation.2 | custom fusion | bytes 37773312 | tf_op jit(solution)/shard_map/gather | solution.py:60
  2294.8 29.4 reshape.385
  2338.5 67.3 %multiply_reduce_fusion = f32[1024,1536]{1,0:T(8,128)} fusion(bf16[1024,6,1536]{2,1,0:T(8,128)(2,1)} %reshape.385, f32[1024,6]{1,0:T(8,128)} %copy.50), kind=kLoop, calls=%fused_computation.9 | loop fusion | flops 26738688 | bytes 25190400 | tf_op jit(solution)/shard_map/reduce_sum | solution.py:61
  2412.3 47.1 %reshape.296 = bf16[12224,1536]{1,0:T(8,128)(2,1)} reshape(bf16[64,191,1536]{2,1,0:T(8,128)(2,1)} %all-to-all-done.3) | data formatting | bytes 75104256 | tf_op jit(solution)/shard_map/reshape | solution.py:84
  2459.4 131.5 %gather_fusion.5 = bf16[6144,1536]{1,0:T(8,128)(2,1)} fusion(bf16[12224,1536]{1,0:T(8,128)(2,1)} %reshape.296, s32[6144]{0:T(1024)S(1)} %broadcast_clamp_fusion), kind=kCustom, calls=%fused_computation.5 | custom fusion | bytes 37773312 | tf_op jit(solution)/shard_map/gather | solution.py:84
  2590.8 31.9 %reshape.432 = f32[1024,6,1536]{2,1,0:T(8,128)} reshape(bf16[6144,1536]{1,0:T(8,128)(2,1)} %gather_fusion.5) | data formatting | bytes 56623104 | tf_op jit(solution)/shard_map/convert_element_type | solution.py:84
  2622.7 27.2 reduce_sum.37
  2658.2 412.8 %all-reduce.9 = (bf16[1024,1536]{1,0:T(8,128)(2,1)}, f32[1024,6]{0,1:T(8,128)S(1)}) all-reduce(f32[1024,1536]{1,0:T(8,128)} %convolution_add_fusion, f32[1024,6]{0,1:T(8,128)S(1)} %bitcast.197), channel_id=1, replica_groups=mesh['etp'=4,'ep'=8] {'etp'}, use_global_device_ids=true, to_apply=%region_6.7 | all-reduce | flops 1579008 | bytes 9486336 | tf_op jit(solution)/shard_map/psum | solution.py:68
  (148 shorter events, 201.1 us)
Async XLA Ops:
  8.0 1106.9 %copy-start = (bf16[8,128,1536]{2,1,0:T(8,128)(2,1)S(1)}, bf16[8,128,1536]{2,1,0:T(8,128)(2,1)}, u32[]{:S(2)}) copy-start(bf16[8,128,1536]{2,1,0:T(8,128)(2,1)} %param.15) | copy-start | bytes 9437188
  11.3 52.4 %copy-start.28 = (s32[6144]{0:T(1024)}, s32[6144]{0:T(1024)S(1)}, u32[]{:S(2)}) copy-start(s32[6144]{0:T(1024)S(1)} %reshape.286) | copy-start | bytes 73732
  12.8 43.3 %copy-start.30 = (s32[6144,1]{0,1:T(1,128)}, s32[6144,1]{0,1:T(1,128)S(1)}, u32[]{:S(2)}) copy-start(s32[6144,1]{0,1:T(1,128)S(1)} %reshape.285) | copy-start | bytes 73732
  63.8 67.7 %copy-start.2 = (s32[6144]{0:T(1024)}, s32[6144]{0:T(1024)S(1)}, u32[]{:S(2)}) copy-start(s32[6144]{0:T(1024)S(1)} %get-tuple-element.11) | copy-start | bytes 73732
  281.1 7.9 copy-start.25
  281.2 10.9 copy-start.27
  281.2 417.4 %all-to-all-start = ((bf16[64,191,1536]{2,1,0:T(8,128)(2,1)}), bf16[64,191,1536]{2,1,0:T(8,128)(2,1)}, u32[]{:S(2)}, u32[]{:S(2)}) async-start(bf16[64,191,1536]{2,1,0:T(8,128)(2,1)} %broadcast_select_fusion), calls=%async_computation | async-start | bytes 75497472 | tf_op jit(solution)/shard_map/all_to_all | solution.py:53
  436.0 56.6 %copy-start.37 = (s32[64]{0:T(128)S(1)}, s32[64]{0:T(128)}, u32[]{:S(2)}) copy-start(s32[64]{0:T(128)} %copy-done.36) | copy-start | bytes 772
  698.6 416.3 %all-to-all-start.2 = ((bf16[64,191,1536]{2,1,0:T(8,128)(2,1)}), bf16[64,191,1536]{2,1,0:T(8,128)(2,1)}, u32[]{:S(2)}, u32[]{:S(2)}) async-start(bf16[64,191,1536]{2,1,0:T(8,128)(2,1)} %multiply_convert_fusion), calls=%async_computation.2 | async-start | bytes 75497472 | tf_op jit(solution)/shard_map/all_to_all | solution.py:75
  706.1 19.9 copy-start.9
  1234.0 7.7 copy-start.10
  1234.0 416.6 %all-to-all-start.1 = ((bf16[64,191,1536]{2,1,0:T(8,128)(2,1)}), bf16[64,191,1536]{2,1,0:T(8,128)(2,1)}, u32[]{:S(2)}, u32[]{:S(2)}) async-start(bf16[64,191,1536]{2,1,0:T(8,128)(2,1)} %copy.49), calls=%async_computation.1 | async-start | bytes 75497472 | tf_op jit(solution)/shard_map/all_to_all | solution.py:59
  1380.9 277.7 %copy-start.4 = (bf16[1024,1536]{1,0:T(8,128)(2,1)S(1)}, bf16[1024,1536]{1,0:T(8,128)(2,1)}, u32[]{:S(2)}) copy-start(bf16[1024,1536]{1,0:T(8,128)(2,1)} %param.10) | copy-start | bytes 9437188
  1650.6 761.7 %all-to-all-start.3 = ((bf16[64,191,1536]{2,1,0:T(8,128)(2,1)}), bf16[64,191,1536]{2,1,0:T(8,128)(2,1)}, u32[]{:S(2)}, u32[]{:S(2)}) async-start(bf16[64,191,1536]{2,1,0:T(8,128)(2,1)} %copy.55), calls=%async_computation.3 | async-start | bytes 75497472 | tf_op jit(solution)/shard_map/all_to_all | solution.py:83
  1658.1 394.3 %all-reduce.8.cloned.1.call-start = ((), (), s32[]{:S(2)}) async-start(), calls=%async_computation.5 | async-start | bytes 9437184 | tf_op jit(solution)/shard_map/psum | solution.py:90
  1667.5 9.0 copy-start.14
  1667.5 11.9 copy-start.31
  1667.5 20.7 copy-start.29
  1667.5 57.7 %copy-start.33 = (f32[1024]{0:T(1024)S(1)}, f32[1024]{0:T(1024)}, u32[]{:S(2)}) copy-start(f32[1024]{0:T(1024)} %copy-done.32) | copy-start | bytes 12292
  1667.5 58.3 %copy-start.8 = (bf16[1024,256]{1,0:T(8,128)(2,1)S(1)}, bf16[1024,256]{1,0:T(8,128)(2,1)}, u32[]{:S(2)}) copy-start(bf16[1024,256]{1,0:T(8,128)(2,1)} %copy-done.7) | copy-start | bytes 1572868
  1667.5 58.3 %copy-start.22 = (bf16[1536,256]{1,0:T(8,128)(2,1)S(1)}, bf16[1536,256]{1,0:T(8,128)(2,1)}, u32[]{:S(2)}) copy-start(bf16[1536,256]{1,0:T(8,128)(2,1)} %param.16) | copy-start | bytes 2359300
  1669.7 1403.1 %all-reduce.6.cloned.1.call-start = ((), (), s32[]{:S(2)}) async-start(), calls=%async_computation.4 | async-start | bytes 12582912 | tf_op jit(solution)/shard_map/psum | solution.py:93
  1729.5 329.0 %copy-start.12 = (bf16[8,8,191,128]{3,2,0,1:T(8,128)(2,1)S(1)}, bf16[8,8,191,128]{3,2,0,1:T(8,128)(2,1)}, u32[]{:S(2)}) copy-start(bf16[8,8,191,128]{3,2,0,1:T(8,128)(2,1)} %get-tuple-element.106) | copy-start | bytes 9388036
  2075.4 20.9 copy-start.11
  2294.8 29.4 copy-start.6
  2338.5 67.3 %copy-start.18 = (bf16[1024,256]{1,0:T(8,128)(2,1)S(1)}, bf16[1024,256]{1,0:T(8,128)(2,1)}, u32[]{:S(2)}) copy-start(bf16[1024,256]{1,0:T(8,128)(2,1)} %copy-done.17) | copy-start | bytes 1572868
  2338.5 67.3 %copy-start.24 = (bf16[256,1536]{1,0:T(8,128)(2,1)S(1)}, bf16[256,1536]{1,0:T(8,128)(2,1)}, u32[]{:S(2)}) copy-start(bf16[256,1536]{1,0:T(8,128)(2,1)} %param.18) | copy-start | bytes 2359300
  2622.7 27.2 copy-start.16
  2622.7 27.2 copy-start.21
  2658.1 412.8 %copy-start.26 = (f32[1024,6]{0,1:T(8,128)S(1)}, f32[1024,6]{0,1:T(8,128)}, u32[]{:S(2)}) copy-start(f32[1024,6]{0,1:T(8,128)} %param.12) | copy-start | bytes 73732
  2658.1 412.8 %copy-start.35 = (f32[1024]{0:T(1024)S(1)}, f32[1024]{0:T(1024)}, u32[]{:S(2)}) copy-start(f32[1024]{0:T(1024)} %multiply_divide_fusion.1) | copy-start | bytes 12292
  2658.1 412.8 %copy-start.34 = (f32[1024]{0:T(1024)S(1)}, f32[1024]{0:T(1024)}, u32[]{:S(2)}) copy-start(f32[1024]{0:T(1024)} %copy-done.32) | copy-start | bytes 12292
  (12 other events, 39.8 us)
Sparse Core Ops, SparseCore 0:
  1669.8 382.5 all-reduce.7
Sparse Core Ops, SparseCore 1:
  2658.2 414.5 all-reduce.5
where the time goes:
time: 3100 us; the launch traced here: 3090 us
  waiting for transfers between devices  1130 us (36%)
  local copies, waits for them, and re-layouts  985 us (32%)
  blocking collectives  413 us (13%)
  other arithmetic  261 us (8%)
  matrix products  249 us (8%)
  starting transfers between devices  31 us (1%)
    psum x1, blocking collectives, device_step(): y_out = lax.psum(routed + shared_out, 'etp').astype(jnp.bfloat16)  413 us
    all_to_all x1, waiting for transfers between devices, device_step(): lax.all_to_all(dy_send, 'ep', 0, 0, tiled=True).reshape(buffer_shape)  370 us
    psum x1, waiting for transfers between devices, device_step(): lax.psum(jnp.einsum('td,tf->df', x_local, shared_da, preferred_element_ty...  323 us
    all_to_all x1, waiting for transfers between devices, device_step(): lax.all_to_all(part_out.reshape(num_experts, capacity, hidden_dim), 'ep',...  270 us
    all_to_all x1, waiting for transfers between devices, device_step(): lax.all_to_all(x_send, 'ep', 0, 0, tiled=True).reshape(buffer_shape)  169 us
    gather x2, local copies, waits for them, and re-layouts, device_step(): out_rows = out_back.reshape(num_experts * capacity, hidden_dim)[entry_slot]  161 us
    gather x1, local copies, waits for them, and re-layouts, device_step(): dx_back.reshape(num_experts * capacity, hidden_dim)[entry_slot]  131 us
    gather x2, local copies, waits for them, and re-layouts, device_step(): x_local[slot_token]  123 us
  transfers between devices with their start and end apart: 6, of which 5 were waited for; matrix products, arithmetic and copies ran while one was open for 27% of the time, Pallas kernels for 0%

commit v1 on v0

v1 whole, which is shorter than its diff:
```python
import functools

import jax
import jax.numpy as jnp
from jax import lax
from jax.experimental import pallas as pl
from jax.experimental.pallas import tpu as pltpu
from jax.sharding import PartitionSpec as P

ROUTE_SCALE = 2.5
ROW_TILE = 256


def gate_weights(scores):
    return ROUTE_SCALE * scores / jnp.sum(scores, axis=-1, keepdims=True)


def forward_kernel(num_exp, num_adds, gated, packed, num_deps, *refs):
    x_ref, g_ref, wgu_ref, wd_ref = refs[:4]
    adds = refs[4:4 + num_adds]
    outs = refs[4 + num_adds + num_deps:]
    y_ref, ab_ref, gh_ref = outs[:3]
    x = x_ref[...]
    gh_parts = []
    for e in range(num_exp):
        ab = jnp.dot(x, wgu_ref[e], preferred_element_type=jnp.float32)
        ab_ref[:, e * 256:(e + 1) * 256] = ab
        a, b = ab[:, :128], ab[:, 128:]
        hidden = (a * jax.nn.sigmoid(a) * b).astype(jnp.bfloat16)
        if gated:
            gate = jnp.broadcast_to(g_ref[0, :, e:e + 1], a.shape)
            hidden = jnp.where(gate != 0.0, gate * hidden.astype(jnp.float32), 0.0).astype(jnp.bfloat16)
        gh_ref[:, e * 128:(e + 1) * 128] = hidden
        gh_parts.append(hidden)
    y = jnp.dot(jnp.concatenate(gh_parts, axis=1), wd_ref[...], preferred_element_type=jnp.float32)
    for add in adds:
        y = y + add[...].astype(jnp.float32)
    y_ref[...] = y.astype(y_ref.dtype)
    if packed:
        outs[3][...] = x


def backward_kernel(num_exp, num_adds, gated, packed, num_deps, *refs):
    dy_ref, g_ref, ab_ref, wdt_ref, wgut_ref = refs[:5]
    adds = refs[5:5 + num_adds]
    outs = refs[5 + num_adds + num_deps:]
    dx_ref, dg_ref, dab_ref = outs[:3]
    dy = dy_ref[...]
    lane = lax.broadcasted_iota(jnp.int32, dg_ref.shape, 1)
    dg = jnp.zeros(dg_ref.shape, jnp.float32)
    dab_parts = []
    for e in range(num_exp):
        if e % 2 == 0:
            d_pair = jnp.dot(dy, wdt_ref[:, e * 128:(e + 2) * 128], preferred_element_type=jnp.float32)
        d_e = d_pair[:, (e % 2) * 128:(e % 2 + 1) * 128]
        a, b = ab_ref[:, e * 256:e * 256 + 128], ab_ref[:, e * 256 + 128:(e + 1) * 256]
        logistic = jax.nn.sigmoid(a)
        silu_val = a * logistic
        silu_grad = logistic * (1.0 + a * (1.0 - logistic))
        if gated:
            hidden = (silu_val * b).astype(jnp.bfloat16).astype(jnp.float32)
            score = jnp.sum(hidden * d_e, axis=1, keepdims=True)
            dg = dg + jnp.where(lane == e, score, 0.0)
            gate = jnp.broadcast_to(g_ref[0, :, e:e + 1], a.shape)
            live = gate != 0.0
            dh = gate * d_e
            da = jnp.where(live, dh * b * silu_grad, 0.0)
            db = jnp.where(live, dh * silu_val, 0.0)
        else:
            da = d_e * b * silu_grad
            db = d_e * silu_val
        dab = jnp.concatenate([da.astype(jnp.bfloat16), db.astype(jnp.bfloat16)], axis=1)
        dab_ref[:, e * 256:(e + 1) * 256] = dab
        dab_parts.append(dab)
    dx = jnp.dot(jnp.concatenate(dab_parts, axis=1), wgut_ref[...], preferred_element_type=jnp.float32)
    for add in adds:
        dx = dx + add[...].astype(jnp.float32)
    dx_ref[...] = dx.astype(dx_ref.dtype)
    dg_ref[...] = dg
    if packed:
        outs[3][...] = dy


def whole_spec(arr):
    return pl.BlockSpec(arr.shape, lambda t: (0,) * len(arr.shape), pipeline_mode=pl.Buffered(1))


def row_tiles(rows, cols, base=0):
    tile = min(ROW_TILE, rows)
    return pl.BlockSpec((tile, cols), lambda t: (base * (rows // tile) + t, 0))


def gate_spec(rows, flip):
    return pl.BlockSpec((1, min(ROW_TILE, rows), 8), lambda t: (flip, t, 0))


def run_kernel(body, rows, arrays, specs, bufs, deps, outs, buf_outs, flops):
    any_spec = pl.BlockSpec(memory_space=pl.ANY)
    extra = list(bufs) + list(deps)
    aliases = {}
    for k, buf in enumerate(bufs):
        aliases[len(arrays) + k] = len(outs) - len(buf_outs) + k
    all_outs = outs
    return pl.pallas_call(
        functools.partial(body, len(extra)),
        grid=(rows // min(ROW_TILE, rows),),
        in_specs=list(specs) + [any_spec] * len(extra),
        out_specs=[spec for _, _, spec in all_outs],
        out_shape=[jax.ShapeDtypeStruct(shape, dtype) for shape, dtype, _ in all_outs],
        input_output_aliases=aliases,
        compiler_params=pltpu.CompilerParams(dimension_semantics=('arbitrary',), vmem_limit_bytes=56 * 1024 * 1024),
        cost_estimate=pl.CostEstimate(flops=flops, bytes_accessed=flops // 1000, transcendentals=0),
    )(*arrays, *extra)


def forward_pass(x, gates, flip, weights, adds=(), bufs=None, deps=(), out_dtype=jnp.bfloat16, shards=0):
    wgu, wd = weights
    rows, hidden = x.shape
    num_exp = wgu.shape[0]
    gated = gates is not None
    if not gated:
        gates, flip = jnp.zeros((1, rows, 8), jnp.float32), 0
    tile = row_tiles(rows, hidden)
    arrays = [x, gates, wgu, wd, *adds]
    specs = [tile, gate_spec(rows, flip), whole_spec(wgu), whole_spec(wd)] + [tile] * len(adds)
    slot = flip if shards else 0
    outs = [((rows, hidden), out_dtype, tile), ((rows, num_exp * 256), jnp.float32, row_tiles(rows, num_exp * 256)),
            ((max(shards, 1) * rows, num_exp * 128), jnp.bfloat16, row_tiles(rows, num_exp * 128, slot))]
    buf_outs = []
    if shards:
        outs.append(((shards * rows, hidden), jnp.bfloat16, row_tiles(rows, hidden, slot)))
        buf_outs = outs[2:]
    body = lambda num_deps, *refs: forward_kernel(num_exp, len(adds), gated, bool(shards), num_deps, *refs)
    return run_kernel(body, rows, arrays, specs, bufs or (), deps, outs, buf_outs, 6 * rows * hidden * 128 * num_exp)


def backward_pass(dy, gates, flip, ab, weights, adds=(), bufs=None, deps=(), out_dtype=jnp.bfloat16, shards=0):
    wdt, wgut = weights
    rows, hidden = dy.shape
    num_exp = wdt.shape[1] // 128
    gated = gates is not None
    if not gated:
        gates, flip = jnp.zeros((1, rows, 8), jnp.float32), 0
    tile = row_tiles(rows, hidden)
    arrays = [dy, gates, ab, wdt, wgut, *adds]
    specs = [tile, gate_spec(rows, flip), row_tiles(rows, num_exp * 256), whole_spec(wdt), whole_spec(wgut)] + [tile] * len(adds)
    slot = flip if shards else 0
    outs = [((rows, hidden), out_dtype, tile), ((rows, 8), jnp.float32, row_tiles(rows, 8)),
            ((max(shards, 1) * rows, num_exp * 256), jnp.bfloat16, row_tiles(rows, num_exp * 256, slot))]
    buf_outs = []
    if shards:
        outs.append(((shards * rows, hidden), jnp.bfloat16, row_tiles(rows, hidden, slot)))
        buf_outs = outs[2:]
    body = lambda num_deps, *refs: backward_kernel(num_exp, len(adds), gated, bool(shards), num_deps, *refs)
    return run_kernel(body, rows, arrays, specs, bufs or (), deps, outs, buf_outs, 8 * rows * hidden * 128 * num_exp)


def pack_weights(wg, wu, wd):
    num_exp, hidden, _ = wg.shape
    wgu = jnp.concatenate([wg, wu], axis=2)
    wgut = wgu.transpose(0, 2, 1).reshape(num_exp * 256, hidden)
    wd2 = wd.reshape(num_exp * 128, hidden)
    return (wgu, wd2), (wd2.T, wgut)


def solution(mesh):
    ep_size = mesh.shape['ep']
    etp_size = mesh.shape['etp']
    row_spec = P('ep', None)
    col_spec = P('ep', None, 'etp')
    down_spec = P('ep', 'etp', None)
    in_specs = (row_spec, row_spec, row_spec, col_spec, col_spec, down_spec, P(None, 'etp'), P(None, 'etp'), P('etp', None), row_spec)
    out_specs = (row_spec, row_spec, row_spec, col_spec, col_spec, down_spec, P(None, 'etp'), P(None, 'etp'), P('etp', None))

    def send(value, flip):
        return lax.ppermute(value, 'ep', [(i, i ^ flip) for i in range(ep_size)])

    def block_step(x_local, ids_local, scores_local, wg_local, wu_local, wd_local, sg_local, su_local, sd_local, dy_local):
        rows, _ = ids_local.shape
        hidden = x_local.shape[1]
        local_experts = wg_local.shape[0]
        num_experts = local_experts * ep_size
        me = lax.axis_index('ep')
        flips = me ^ jnp.arange(ep_size)
        quarter = rows // etp_size

        gates = gate_weights(scores_local)
        chosen = ids_local.T[:, None, :] == jnp.arange(num_experts)[None, :, None]
        gate_rows = jnp.sum(jnp.where(chosen, gates.T[:, None, :], 0.0), axis=0)
        gate_recv = lax.all_to_all(gate_rows, 'ep', 0, 0, tiled=True)
        gate_recv = gate_recv.reshape(ep_size, local_experts, rows)[flips].transpose(0, 2, 1)

        def share(local):
            mine = lax.dynamic_slice_in_dim(local, lax.axis_index('etp') * quarter, quarter, axis=0)
            got = {0: local}
            corner = send(mine, 6)
            for f in (1, 2, 4):
                got[f] = send(local, f)
            got[6] = lax.all_gather(corner, 'etp', axis=0, tiled=True)
            for f in (3, 5, 7):
                got[f] = send(got[f ^ 1], 1)
            return got

        x, dy = share(x_local), share(dy_local)

        split = lambda mat: mat.reshape(hidden, 2, 128).transpose(1, 0, 2)
        shared_fwd, shared_bwd = pack_weights(split(sg_local), split(su_local), sd_local.reshape(2, 128, hidden))
        routed_fwd, routed_bwd = pack_weights(wg_local, wu_local, wd_local)

        y_sh, ab_sh, gh_sh = forward_pass(x_local, None, 0, shared_fwd)
        dx_sh, _, dab_sh = backward_pass(dy_local, None, 0, ab_sh, shared_bwd)

        ab, dg, y_back, dx_back = {}, {}, {}, {}
        bufs, deps = None, (dx_sh,)
        for f in (1, 3, 5, 7):
            y_f, ab[f], *bufs = forward_pass(x[f], gate_recv, f, routed_fwd, (), bufs, deps, shards=ep_size)
            deps = ()
            adds = (send(y_f, 1),) + ((y_sh,) if f == 1 else ())
            f -= 1
            y_f, ab[f], *bufs = forward_pass(x[f], gate_recv, f, routed_fwd, adds, bufs, shards=ep_size)
            y_back[f] = send(y_f, f) if f else y_f
        gh_all, x_all = bufs

        def etp_exchange(parts):
            total = sum(parts[f].astype(jnp.float32) for f in (0, 2, 4, 6)).astype(jnp.bfloat16)
            pieces = lax.all_to_all(total, 'etp', 0, 0, tiled=True)
            return jnp.sum(pieces.reshape(etp_size, quarter, hidden).astype(jnp.float32), axis=0)

        y_piece = etp_exchange(y_back).astype(jnp.bfloat16)
        y_out = lax.all_gather(y_piece, 'etp', axis=0, tiled=True)

        bufs, deps = None, (gh_all,)
        for f in (7, 5, 3, 1):
            dx_f, dg[f], *bufs = backward_pass(dy[f], gate_recv, f, ab[f], routed_bwd, (), bufs, deps, shards=ep_size)
            deps = ()
            adds = (send(dx_f, 1),) + ((dx_sh,) if f == 1 else ())
            f -= 1
            dx_f, dg[f], *bufs = backward_pass(dy[f], gate_recv, f, ab[f], routed_bwd, adds, bufs,
                                               (y_piece,) if f == 0 else (), shards=ep_size)
            dx_back[f] = send(dx_f, f) if f else dx_f
        dab_all, dy_all = bufs

        dx_norm = lax.all_gather(etp_exchange(dx_back), 'etp', axis=0, tiled=True)

        dg_send = jnp.stack([dg[f].T for f in range(ep_size)])[flips].reshape(num_experts, rows)
        dg_all = lax.all_to_all(dg_send, 'ep', 0, 0, tiled=True)
        gate_grad = jnp.sum(jnp.where(chosen, dg_all[None], 0.0), axis=1)
        gate_grad = lax.psum(gate_grad, 'etp').T
        _, gate_pull = jax.vjp(gate_weights, scores_local)
        d_scores = gate_pull(gate_grad)[0]

        def up_grads(xs, dabs):
            grad = jnp.einsum('td,tc->dc', xs, dabs, preferred_element_type=jnp.float32)
            return grad.reshape(hidden, dabs.shape[1] // 256, 2, 128)

        def down_grad(ghs, dys):
            return jnp.einsum('tc,td->cd', ghs, dys, preferred_element_type=jnp.float32)

        dws_gu = up_grads(x_local, dab_sh).transpose(2, 0, 1, 3).reshape(2, hidden, 256)
        dws_down = down_grad(gh_sh, dy_local)
        dws_gate, dws_up, dws_down = lax.psum((dws_gu[0], dws_gu[1], dws_down), 'ep')

        dw_gu = up_grads(x_all, dab_all)
        dw_down = down_grad(gh_all, dy_all).reshape(local_experts, 128, hidden)
        dw_gate, dw_up = dw_gu[:, :, 0].transpose(1, 0, 2), dw_gu[:, :, 1].transpose(1, 0, 2)
        return (y_out, dx_norm, d_scores, dw_gate, dw_up, dw_down, dws_gate, dws_up, dws_down)

    return jax.shard_map(block_step, mesh=mesh, in_specs=in_specs, out_specs=out_specs, check_vma=False)
```

time: 3100 us -> 1130 us (0.36)
  local copies, waits for them, and re-layouts: 985 us -> 105 us
  waiting for transfers between devices: 1130 us -> 524 us
  blocking collectives: 413 us -> 15.8 us
  Pallas kernels: 0 us -> 291 us
  other arithmetic: 261 us -> 26.5 us
  matrix products: 249 us -> 102 us
    gather x14 -> x3, local copies, waits for them, and re-layouts: 629 us -> 4.63 us  [the longest x2 3.23 us: block_step(): gate_recv.reshape(ep_size, local_experts, rows)[flips].transpose(0, 2, 1)]
    all_to_all x4, waiting for transfers between devices: 809 us -> 189 us  [the longest x2 151 us: etp_exchange(): pieces = lax.all_to_all(total, 'etp', 0, 0, tiled=True)]
    psum x1, blocking collectives: 413 us -> 15.8 us  [block_step(): gate_grad = lax.psum(gate_grad, 'etp').T]
    psum x2 -> x1, waiting for transfers between devices: 324 us -> 0.01 us  [block_step(): lax.psum((dws_gu[0], dws_gu[1], dws_down), 'ep')]
    pallas_call x0 -> x18, Pallas kernels: none -> 291 us  [run_kernel(): pl.pallas_call(functools.partial(body, len(extra)), grid=(rows // min(ROW...]
    ppermute x0 -> x28, waiting for transfers between devices: none -> 280 us  [send(): return lax.ppermute(value, 'ep', [(i, i ^ flip) for i in range(ep_size)])]
    convert_element_type x4 -> x0, local copies, waits for them, and re-layouts: 158 us -> none  [the longest x1 56.6 us: device_step(): slot_gate[:, :, None] * dy_local[slot_token]]
    reshape x8 -> x4, local copies, waits for them, and re-layouts: 177 us -> 20.6 us  [the longest x1 17 us: up_grads(): return grad.reshape(hidden, dabs.shape[1] // 256, 2, 128)]
  transfers between devices with their start and end apart: 6 -> 37, of which waited for: 5 -> 13; matrix products, arithmetic and copies ran while one was open for 27% -> 18% of each run, Pallas kernels for 0% -> 26%
where the time goes in v1:
time: 1130 us; the launch traced here: 1120 us
  waiting for transfers between devices  524 us (46%)
  Pallas kernels  291 us (26%)
  local copies, waits for them, and re-layouts  105 us (9%)
  matrix products  102 us (9%)
  starting transfers between devices  37.3 us (3%)
  other arithmetic  26.5 us (2%)
  between operations  16 us (1%)
  blocking collectives  15.8 us (1%)
    pallas_call x18, Pallas kernels, run_kernel(): pl.pallas_call(functools.partial(body, len(extra)), grid=(rows // min(ROW...  291 us
    ppermute x28, waiting for transfers between devices, send(): return lax.ppermute(value, 'ep', [(i, i ^ flip) for i in range(ep_size)])  280 us
    all_to_all x2, waiting for transfers between devices, etp_exchange(): pieces = lax.all_to_all(total, 'etp', 0, 0, tiled=True)  151 us
    dot_general x2, matrix products, up_grads(): grad = jnp.einsum('td,tc->dc', xs, dabs, preferred_element_type=jnp.float32)  65.1 us
    all_gather x2, waiting for transfers between devices, share(): got[6] = lax.all_gather(corner, 'etp', axis=0, tiled=True)  54.6 us
    all_to_all x1, waiting for transfers between devices, block_step(): gate_recv = lax.all_to_all(gate_rows, 'ep', 0, 0, tiled=True)  37.6 us
    dot_general x2, matrix products, down_grad(): return jnp.einsum('tc,td->cd', ghs, dys, preferred_element_type=jnp.float32)  37.4 us
    unnamed x76, local copies, waits for them, and re-layouts  31.6 us
  transfers between devices with their start and end apart: 37, of which 13 were waited for; matrix products, arithmetic and copies ran while one was open for 18% of the time, Pallas kernels for 26%

profile of v1, /device:TPU:0, one launch (start us, length us, event | category | flops | bytes accessed | tf_op | source)
XLA Modules:
  0.0 1117.8 jit_solution(13770074413649616846)
XLA Ops:
  46.5 37.6 %all-to-all-done = f32[8,8,1024]{2,1,0:T(8,128)S(1)} async-done(((f32[8,8,1024]{2,1,0:T(8,128)}), f32[8,8,1024]{2,1,0:T(8,128)S(1)}, u32[]{:S(2)}, u32[]{:S(2)}) %all-to-all-start) | async-done | bytes 262176 | tf_op jit(solution)/shard_map/all_to_all | solution.py:190
  87.3 15.9 %shard_map.171 = (bf16[1024,1536]{1,0:T(8,128)(2,1)}, f32[1024,2048]{1,0:T(8,128)}, bf16[8192,1024]{1,0:T(8,128)(2,1)}, bf16[8192,1536]{1,0:T(8,128)(2,1)}) custom-call(bf16[1024,1536]{1,0:T(8,128)(2,1)} %collective-permute-done.refs_0_, f32[8,1024,8]{2,1,0:T(8,128)} %bitcast.76, bf16[8,1536,256]{2,1,0:T(8,128)(2,1)} %constant_dynamic-update-slice_fusion.refs_2_, ...), custom_call_target="tpu_custom_call" | custom-call | flops 9663676416 | bytes 9663676 | tf_op jit(solution)/shard_map/pallas_call | solution.py:104
  110.8 16.6 %shard_map.172 = (bf16[1024,1536]{1,0:T(8,128)(2,1)}, f32[1024,2048]{1,0:T(8,128)}, bf16[8192,1024]{1,0:T(8,128)(2,1)}, bf16[8192,1536]{1,0:T(8,128)(2,1)}) custom-call(bf16[1024,1536]{1,0:T(8,128)(2,1)} %refs_0_.6, f32[8,1024,8]{2,1,0:T(8,128)} %bitcast.77, ...), custom_call_target="tpu_custom_call", output_to_operand_aliasing={{2}: (6, {}), {3}: (7, {})} | custom-call | flops 9663676416 | bytes 9663676 | tf_op jit(solution)/shard_map/pallas_call | solution.py:104
  129.1 15.9 %shard_map.173 = (bf16[1024,1536]{1,0:T(8,128)(2,1)}, f32[1024,2048]{1,0:T(8,128)}, bf16[8192,1024]{1,0:T(8,128)(2,1)}, bf16[8192,1536]{1,0:T(8,128)(2,1)}) custom-call(bf16[1024,1536]{1,0:T(8,128)(2,1)} %copy-done.10, f32[8,1024,8]{2,1,0:T(8,128)} %bitcast.78, ...), custom_call_target="tpu_custom_call", output_to_operand_aliasing={{2}: (4, {}), {3}: (5, {})} | custom-call | flops 9663676416 | bytes 9663676 | tf_op jit(solution)/shard_map/pallas_call | solution.py:104
  148.0 43.1 %collective-permute-done.6.refs_0_ = bf16[1024,1536]{1,0:T(8,128)(2,1)} collective-permute-done((bf16[1024,1536]{1,0:T(8,128)(2,1)}, bf16[1024,1536]{1,0:T(8,128)(2,1)}, u32[]{:S(2)}, u32[]{:S(2)}) %collective-permute-start.6) | collective-permute-done | bytes 3145760 | tf_op jit(solution)/shard_map/ppermute | solution.py:176
  191.6 16.2 %shard_map.174 = (bf16[1024,1536]{1,0:T(8,128)(2,1)}, f32[1024,2048]{1,0:T(8,128)}, bf16[8192,1024]{1,0:T(8,128)(2,1)}, bf16[8192,1536]{1,0:T(8,128)(2,1)}) custom-call(bf16[1024,1536]{1,0:T(8,128)(2,1)} %collective-permute-done.2.refs_0_, f32[8,1024,8]{2,1,0:T(8,128)} %bitcast.79, ...), custom_call_target="tpu_custom_call", output_to_operand_aliasing={{2}: (5, {}), {3}: (6, {})} | custom-call | flops 9663676416 | bytes 9663676 | tf_op jit(solution)/shard_map/pallas_call | solution.py:104
  209.5 16.0 %shard_map.175 = (bf16[1024,1536]{1,0:T(8,128)(2,1)}, f32[1024,2048]{1,0:T(8,128)}, bf16[8192,1024]{1,0:T(8,128)(2,1)}, bf16[8192,1536]{1,0:T(8,128)(2,1)}) custom-call(bf16[1024,1536]{1,0:T(8,128)(2,1)} %copy-done.7, f32[8,1024,8]{2,1,0:T(8,128)} %bitcast.80, ...), custom_call_target="tpu_custom_call", output_to_operand_aliasing={{2}: (4, {}), {3}: (5, {})} | custom-call | flops 9663676416 | bytes 9663676 | tf_op jit(solution)/shard_map/pallas_call | solution.py:104
  229.6 25.6 %all-gather.5.cloned.1.call-done.refs_0_ = bf16[1024,1536]{1,0:T(8,128)(2,1)} async-done(((bf16[256,1536]{1,0:T(8,128)(2,1)}), bf16[1024,1536]{1,0:T(8,128)(2,1)}) %all-gather.5.cloned.1.call-update) | async-done | bytes 3145744 | tf_op jit(solution)/shard_map/all_gather | solution.py:199
  255.2 16.3 %shard_map.176 = (bf16[1024,1536]{1,0:T(8,128)(2,1)}, f32[1024,2048]{1,0:T(8,128)}, bf16[8192,1024]{1,0:T(8,128)(2,1)}, bf16[8192,1536]{1,0:T(8,128)(2,1)}) custom-call(bf16[1024,1536]{1,0:T(8,128)(2,1)} %collective-permute-done.6.refs_0_, f32[8,1024,8]{2,1,0:T(8,128)} %bitcast.81, ...), custom_call_target="tpu_custom_call", output_to_operand_aliasing={{2}: (5, {}), {3}: (6, {})} | custom-call | flops 9663676416 | bytes 9663676 | tf_op jit(solution)/shard_map/pallas_call | solution.py:104
  273.1 16.1 %shard_map.177 = (bf16[1024,1536]{1,0:T(8,128)(2,1)}, f32[1024,2048]{1,0:T(8,128)}, bf16[8192,1024]{1,0:T(8,128)(2,1)}, bf16[8192,1536]{1,0:T(8,128)(2,1)}) custom-call(bf16[1024,1536]{1,0:T(8,128)(2,1)} %copy-done.8, f32[8,1024,8]{2,1,0:T(8,128)} %bitcast.82, ...), custom_call_target="tpu_custom_call", output_to_operand_aliasing={{2}: (4, {}), {3}: (5, {})} | custom-call | flops 9663676416 | bytes 9663676 | tf_op jit(solution)/shard_map/pallas_call | solution.py:104
  289.8 29.0 %all-gather.9.cloned.1.call-done.refs_0_ = bf16[1024,1536]{1,0:T(8,128)(2,1)} async-done(((bf16[256,1536]{1,0:T(8,128)(2,1)}), bf16[1024,1536]{1,0:T(8,128)(2,1)}) %all-gather.9.cloned.1.call-update) | async-done | bytes 3145744 | tf_op jit(solution)/shard_map/all_gather | solution.py:199
  331.8 16.4 %shard_map.178 = (bf16[1024,1536]{1,0:T(8,128)(2,1)}, f32[1024,2048]{1,0:T(8,128)}, bf16[8192,1024]{1,0:T(8,128)(2,1)}, bf16[8192,1536]{1,0:T(8,128)(2,1)}) custom-call(bf16[1024,1536]{1,0:T(8,128)(2,1)} %all-gather.5.cloned.1.call-done.refs_0_, f32[8,1024,8]{2,1,0:T(8,128)} %bitcast.83, ...), custom_call_target="tpu_custom_call", output_to_operand_aliasing={{2}: (5, {}), {3}: (6, {})} | custom-call | flops 9663676416 | bytes 9663676 | tf_op jit(solution)/shard_map/pallas_call | solution.py:104
  348.2 18.2 %shard_map.179 = (bf16[1024,1536]{1,0:T(8,128)(2,1)}, f32[1024,8]{1,0:T(8,128)}, bf16[8192,2048]{1,0:T(8,128)(2,1)}, bf16[8192,1536]{1,0:T(8,128)(2,1)}) custom-call(bf16[1024,1536]{1,0:T(8,128)(2,1)} %collective-permute-done.20.refs_0_, f32[8,1024,8]{2,1,0:T(8,128)} %bitcast.84, f32[1024,2048]{1,0:T(8,128)} %get-tuple-element.110.refs_2_, ...), custom_call_target="tpu_custom_call" | custom-call | flops 12884901888 | bytes 12884901 | tf_op jit(solution)/shard_map/pallas_call | solution.py:104
  366.7 22.9 %collective-permute-done.17.refs_0_ = bf16[1024,1536]{1,0:T(8,128)(2,1)} collective-permute-done((bf16[1024,1536]{1,0:T(8,128)(2,1)}, bf16[1024,1536]{1,0:T(8,128)(2,1)}, u32[]{:S(2)}, u32[]{:S(2)}) %collective-permute-start.17) | collective-permute-done | bytes 3145760 | tf_op jit(solution)/shard_map/ppermute | solution.py:176
  391.1 18.3 %shard_map.180 = (bf16[1024,1536]{1,0:T(8,128)(2,1)}, f32[1024,8]{1,0:T(8,128)}, bf16[8192,2048]{1,0:T(8,128)(2,1)}, bf16[8192,1536]{1,0:T(8,128)(2,1)}) custom-call(bf16[1024,1536]{1,0:T(8,128)(2,1)} %all-gather.9.cloned.1.call-done.refs_0_, f32[8,1024,8]{2,1,0:T(8,128)} %bitcast.85, ...), custom_call_target="tpu_custom_call", output_to_operand_aliasing={{2}: (6, {}), {3}: (7, {})} | custom-call | flops 12884901888 | bytes 12884901 | tf_op jit(solution)/shard_map/pallas_call | solution.py:104
  411.1 18.0 %shard_map.181 = (bf16[1024,1536]{1,0:T(8,128)(2,1)}, f32[1024,8]{1,0:T(8,128)}, bf16[8192,2048]{1,0:T(8,128)(2,1)}, bf16[8192,1536]{1,0:T(8,128)(2,1)}) custom-call(bf16[1024,1536]{1,0:T(8,128)(2,1)} %copy-done.9, f32[8,1024,8]{2,1,0:T(8,128)} %bitcast.86, f32[1024,2048]{1,0:T(8,128)} %get-tuple-element.108.refs_2_, ...), custom_call_target="tpu_custom_call", output_to_operand_aliasing={{2}: (5, {}), {3}: (6, {})} | custom-call | flops 12884901888 | bytes 12884901 | tf_op jit(solution)/shard_map/pallas_call | solution.py:104
  429.5 30.8 %collective-permute-done.15.refs_0_ = bf16[1024,1536]{1,0:T(8,128)(2,1)} collective-permute-done((bf16[1024,1536]{1,0:T(8,128)(2,1)S(1)}, bf16[1024,1536]{1,0:T(8,128)(2,1)}, u32[]{:S(2)}, u32[]{:S(2)}) %collective-permute-start.15) | collective-permute-done | bytes 3145760 | tf_op jit(solution)/shard_map/ppermute | solution.py:176
  463.8 18.5 %shard_map.182 = (bf16[1024,1536]{1,0:T(8,128)(2,1)}, f32[1024,8]{1,0:T(8,128)}, bf16[8192,2048]{1,0:T(8,128)(2,1)}, bf16[8192,1536]{1,0:T(8,128)(2,1)}) custom-call(bf16[1024,1536]{1,0:T(8,128)(2,1)} %collective-permute-done.17.refs_0_, f32[8,1024,8]{2,1,0:T(8,128)} %bitcast.87, ...), custom_call_target="tpu_custom_call", output_to_operand_aliasing={{2}: (6, {}), {3}: (7, {})} | custom-call | flops 12884901888 | bytes 12884901 | tf_op jit(solution)/shard_map/pallas_call | solution.py:104
  484.0 18.0 %shard_map.183 = (bf16[1024,1536]{1,0:T(8,128)(2,1)}, f32[1024,8]{1,0:T(8,128)}, bf16[8192,2048]{1,0:T(8,128)(2,1)}, bf16[8192,1536]{1,0:T(8,128)(2,1)}) custom-call(bf16[1024,1536]{1,0:T(8,128)(2,1)} %copy-done.6, f32[8,1024,8]{2,1,0:T(8,128)} %bitcast.88, f32[1024,2048]{1,0:T(8,128)} %get-tuple-element.106.refs_2_, ...), custom_call_target="tpu_custom_call", output_to_operand_aliasing={{2}: (5, {}), {3}: (6, {})} | custom-call | flops 12884901888 | bytes 12884901 | tf_op jit(solution)/shard_map/pallas_call | solution.py:104
  502.6 29.0 %collective-permute-done.5 = bf16[1024,1536]{1,0:T(8,128)(2,1)} collective-permute-done((bf16[1024,1536]{1,0:T(8,128)(2,1)}, bf16[1024,1536]{1,0:T(8,128)(2,1)}, u32[]{:S(2)}, u32[]{:S(2)}) %collective-permute-start.5) | collective-permute-done | bytes 3145760 | tf_op jit(solution)/shard_map/ppermute | solution.py:176
  531.6 68.1 %collective-permute-done.9 = bf16[1024,1536]{1,0:T(8,128)(2,1)} collective-permute-done((bf16[1024,1536]{1,0:T(8,128)(2,1)}, bf16[1024,1536]{1,0:T(8,128)(2,1)}, u32[]{:S(2)}, u32[]{:S(2)}) %collective-permute-start.9) | collective-permute-done | bytes 3145760 | tf_op jit(solution)/shard_map/ppermute | solution.py:176
  612.8 18.3 %shard_map.184 = (bf16[1024,1536]{1,0:T(8,128)(2,1)}, f32[1024,8]{1,0:T(8,128)}, bf16[8192,2048]{1,0:T(8,128)(2,1)}, bf16[8192,1536]{1,0:T(8,128)(2,1)}) custom-call(bf16[1024,1536]{1,0:T(8,128)(2,1)} %collective-permute-done.15.refs_0_, f32[8,1024,8]{2,1,0:T(8,128)} %bitcast.89, ...), custom_call_target="tpu_custom_call", output_to_operand_aliasing={{2}: (6, {}), {3}: (7, {})} | custom-call | flops 12884901888 | bytes 12884901 | tf_op jit(solution)/shard_map/pallas_call | solution.py:104
  631.1 18.1 %shard_map.185 = (bf16[1024,1536]{1,0:T(8,128)(2,1)}, f32[1024,8]{1,0:T(8,128)}, bf16[8192,2048]{1,0:T(8,128)(2,1)}, bf16[8192,1536]{1,0:T(8,128)(2,1)}) custom-call(bf16[1024,1536]{1,0:T(8,128)(2,1)} %collective-permute-done.14.refs_0_, f32[8,1024,8]{2,1,0:T(8,128)} %bitcast.90, ...), custom_call_target="tpu_custom_call", output_to_operand_aliasing={{2}: (5, {}), {3}: (6, {})} | custom-call | flops 12884901888 | bytes 12884901 | tf_op jit(solution)/shard_map/pallas_call | solution.py:104
  652.9 30.5 %all-to-all-done.1 = bf16[4,256,1536]{2,1,0:T(8,128)(2,1)} async-done(((bf16[4,256,1536]{2,1,0:T(8,128)(2,1)}), bf16[4,256,1536]{2,1,0:T(8,128)(2,1)}, u32[]{:S(2)}, u32[]{:S(2)}) %all-to-all-start.1) | async-done | bytes 3145760 | tf_op jit(solution)/shard_map/all_to_all | solution.py:226
  688.6 19.2 %shard_map.186 = (bf16[1024,1536]{1,0:T(8,128)(2,1)}, f32[1024,8]{1,0:T(8,128)}, bf16[8192,2048]{1,0:T(8,128)(2,1)}, bf16[8192,1536]{1,0:T(8,128)(2,1)}) custom-call(bf16[1024,1536]{1,0:T(8,128)(2,1)} %refs_0_.7, f32[8,1024,8]{2,1,0:T(8,128)} %bitcast.91, f32[1024,2048]{1,0:T(8,128)} %get-tuple-element.103.refs_2_, ...), custom_call_target="tpu_custom_call", output_to_operand_aliasing={{2}: (7, {}), {3}: (8, {})} | custom-call | flops 12884901888 | bytes 12884901 | tf_op jit(solution)/shard_map/pallas_call | solution.py:104
  707.8 13.9 %collective-permute-done.27 = bf16[1024,1536]{1,0:T(8,128)(2,1)} collective-permute-done((bf16[1024,1536]{1,0:T(8,128)(2,1)}, bf16[1024,1536]{1,0:T(8,128)(2,1)}, u32[]{:S(2)}, u32[]{:S(2)}) %collective-permute-start.27) | collective-permute-done | bytes 3145760 | tf_op jit(solution)/shard_map/ppermute | solution.py:176
  721.6 66.8 %collective-permute-done.26 = bf16[1024,1536]{1,0:T(8,128)(2,1)} collective-permute-done((bf16[1024,1536]{1,0:T(8,128)(2,1)}, bf16[1024,1536]{1,0:T(8,128)(2,1)}, u32[]{:S(2)}, u32[]{:S(2)}) %collective-permute-start.26) | collective-permute-done | bytes 3145760 | tf_op jit(solution)/shard_map/ppermute | solution.py:176
  802.3 120.6 %all-to-all-done.2 = bf16[4,256,1536]{2,1,0:T(8,128)(2,1)S(1)} async-done(((bf16[4,256,1536]{2,1,0:T(8,128)(2,1)}), bf16[4,256,1536]{2,1,0:T(8,128)(2,1)S(1)}, u32[]{:S(2)}, u32[]{:S(2)}) %all-to-all-start.2) | async-done | bytes 3145760 | tf_op jit(solution)/shard_map/all_to_all | solution.py:226
  948.9 61.1 %fusion.5 = f32[1536,2048]{1,0:T(8,128)} fusion(bf16[8192,1536]{1,0:T(8,128)(2,1)} %get-tuple-element.142, bf16[8192,2048]{1,0:T(8,128)(2,1)} %get-tuple-element.143), kind=kOutput, calls=%fused_computation.34 | convolution fusion | flops 51539607552 | bytes 71303168 | tf_op jit(solution)/shard_map/td,tc->dc/dot_general | solution.py:253
  1010.0 17.0 %reshape.99 = f32[1536,8,2,128]{3,2,1,0:T(2,128)} reshape(f32[1536,2048]{1,0:T(8,128)} %fusion.5) | data formatting | bytes 25165824 | tf_op jit(solution)/shard_map/reshape | solution.py:254
  1027.0 34.2 %fusion.6 = f32[1024,1536]{1,0:T(8,128)} fusion(bf16[8192,1024]{1,0:T(8,128)(2,1)} %get-tuple-element.111.refs_5_, bf16[8192,1536]{1,0:T(8,128)(2,1)} %get-tuple-element.144), kind=kOutput, calls=%fused_computation.35 | convolution fusion | flops 25769803776 | bytes 48234496 | tf_op jit(solution)/shard_map/tc,td->cd/dot_general | solution.py:257
  1082.1 15.8 %psum.28 = f32[6,1024]{1,0:T(8,128)S(1)} all-reduce(f32[6,1024]{1,0:T(8,128)S(1)} %select_reduce_fusion), channel_id=1, replica_groups=mesh['etp'=4,'ep'=8] {'etp'}, use_global_device_ids=true, to_apply=%region_5.6 | all-reduce | flops 6144 | bytes 49152 | tf_op jit(solution)/shard_map/psum | solution.py:248
  (188 shorter events, 179.8 us)
Async XLA Ops:
  8.0 79.3 %collective-permute-start = (bf16[1024,1536]{1,0:T(8,128)(2,1)}, bf16[1024,1536]{1,0:T(8,128)(2,1)}, u32[]{:S(2)}, u32[]{:S(2)}) collective-permute-start(bf16[1024,1536]{1,0:T(8,128)(2,1)} %refs_0_.6), channel_id=1, source_target_pairs={{0,1},{1,0},{2,3},{3,2},{4,5},{5,4},{6,7},{7,6},{8,9},{9,8},{10,11... | collective-permute-start | bytes 9437192 | tf_op jit(solution)/shard_map/ppermute | solution.py:176
  8.6 94.7 %collective-permute-start.2 = (bf16[1024,1536]{1,0:T(8,128)(2,1)}, bf16[1024,1536]{1,0:T(8,128)(2,1)}, u32[]{:S(2)}, u32[]{:S(2)}) collective-permute-start(bf16[1024,1536]{1,0:T(8,128)(2,1)} %refs_0_.6), channel_id=1, source_target_pairs={{0,2},{1,3},{2,0},{3,1},{4,6},{5,7},{6,4},{7,5},{8,10},{9,11},{10,... | collective-permute-start | bytes 9437192 | tf_op jit(solution)/shard_map/ppermute | solution.py:176
  14.4 69.7 %all-to-all-start = ((f32[8,8,1024]{2,1,0:T(8,128)}), f32[8,8,1024]{2,1,0:T(8,128)S(1)}, u32[]{:S(2)}, u32[]{:S(2)}) async-start(f32[8,8,1024]{2,1,0:T(8,128)} %bitcast.2), calls=%async_computation | async-start | bytes 524288 | tf_op jit(solution)/shard_map/all_to_all | solution.py:190
  17.8 237.4 %all-gather.5.cloned.1.call-start = ((), (), s32[]{:S(2)}) async-start(), calls=%async_computation.4 | async-start | bytes 3932160 | tf_op jit(solution)/shard_map/all_gather | solution.py:199
  103.3 24.1 %collective-permute-start.3 = (bf16[1024,1536]{1,0:T(8,128)(2,1)}, bf16[1024,1536]{1,0:T(8,128)(2,1)S(1)}, u32[]{:S(2)}, u32[]{:S(2)}) collective-permute-start(bf16[1024,1536]{1,0:T(8,128)(2,1)} %collective-permute-done.2.refs_0_), channel_id=1, source_target_pairs={{0,1},{1,0},{2,3},{3,2},{4,5},{5,4},{6,7},{7,6},{8,9},{9,8},{10,11... | collective-permute-start | bytes 9437192 | tf_op jit(solution)/shard_map/ppermute | solution.py:176
  103.8 87.3 %collective-permute-start.6 = (bf16[1024,1536]{1,0:T(8,128)(2,1)}, bf16[1024,1536]{1,0:T(8,128)(2,1)}, u32[]{:S(2)}, u32[]{:S(2)}) collective-permute-start(bf16[1024,1536]{1,0:T(8,128)(2,1)} %refs_0_.6), channel_id=1, source_target_pairs={{0,4},{1,5},{2,6},{3,7},{4,0},{5,1},{6,2},{7,3},{8,12},{9,13},{10,... | collective-permute-start | bytes 9437192 | tf_op jit(solution)/shard_map/ppermute | solution.py:176
  145.0 46.6 %collective-permute-start.4 = (bf16[1024,1536]{1,0:T(8,128)(2,1)}, bf16[1024,1536]{1,0:T(8,128)(2,1)}, u32[]{:S(2)}, u32[]{:S(2)}) collective-permute-start(bf16[1024,1536]{1,0:T(8,128)(2,1)} %get-tuple-element.87), channel_id=1, source_target_pairs={{0,1},{1,0},{2,3},{3,2},{4,5},{5,4},{6,7},{7,6},{8,9},{9,8},{10,11... | collective-permute-start | bytes 9437192 | tf_op jit(solution)/shard_map/ppermute | solution.py:176
  146.4 44.7 %collective-permute-start.10 = (bf16[256,1536]{1,0:T(8,128)(2,1)S(1)}, bf16[256,1536]{1,0:T(8,128)(2,1)}, u32[]{:S(2)}, u32[]{:S(2)}) collective-permute-start(bf16[256,1536]{1,0:T(8,128)(2,1)S(1)} %constant_dynamic-slice_fusion.1), channel_id=1, source_target_pairs={{0,6},{1,7},{2,4},{3,5},{4,2},{5,3},{6,0},{7,1},{8,14},{9,15},{10,... | collective-permute-start | bytes 2359304 | tf_op jit(solution)/shard_map/ppermute | solution.py:176
  191.1 127.7 %all-gather.9.cloned.1.call-start = ((), (), s32[]{:S(2)}) async-start(), calls=%async_computation.6 | async-start | bytes 3932160 | tf_op jit(solution)/shard_map/all_gather | solution.py:199
  225.5 29.7 %collective-permute-start.8 = (bf16[1024,1536]{1,0:T(8,128)(2,1)}, bf16[1024,1536]{1,0:T(8,128)(2,1)}, u32[]{:S(2)}, u32[]{:S(2)}) collective-permute-start(bf16[1024,1536]{1,0:T(8,128)(2,1)} %get-tuple-element.93), channel_id=1, source_target_pairs={{0,1},{1,0},{2,3},{3,2},{4,5},{5,4},{6,7},{7,6},{8,9},{9,8},{10,11... | collective-permute-start | bytes 9437192 | tf_op jit(solution)/shard_map/ppermute | solution.py:176
  228.1 27.0 %collective-permute-start.19 = (bf16[256,1536]{1,0:T(8,128)(2,1)}, bf16[256,1536]{1,0:T(8,128)(2,1)}, u32[]{:S(2)}, u32[]{:S(2)}) collective-permute-start(bf16[256,1536]{1,0:T(8,128)(2,1)} %constant_dynamic-slice_fusion), channel_id=1, source_target_pairs={{0,6},{1,7},{2,4},{3,5},{4,2},{5,3},{6,0},{7,1},{8,14},{9,15},{10,... | collective-permute-start | bytes 2359304 | tf_op jit(solution)/shard_map/ppermute | solution.py:176
  289.3 42.5 %collective-permute-start.12 = (bf16[1024,1536]{1,0:T(8,128)(2,1)}, bf16[1024,1536]{1,0:T(8,128)(2,1)}, u32[]{:S(2)}, u32[]{:S(2)}) collective-permute-start(bf16[1024,1536]{1,0:T(8,128)(2,1)} %get-tuple-element.99), channel_id=1, source_target_pairs={{0,1},{1,0},{2,3},{3,2},{4,5},{5,4},{6,7},{7,6},{8,9},{9,8},{10,11... | collective-permute-start | bytes 9437192 | tf_op jit(solution)/shard_map/ppermute | solution.py:176
  318.8 29.4 %collective-permute-start.20 = (bf16[1024,1536]{1,0:T(8,128)(2,1)}, bf16[1024,1536]{1,0:T(8,128)(2,1)}, u32[]{:S(2)}, u32[]{:S(2)}) collective-permute-start(bf16[1024,1536]{1,0:T(8,128)(2,1)} %all-gather.9.cloned.1.call-done.refs_0_), channel_id=1, source_target_pairs={{0,1},{1,0},{2,3},{3,2},{4,5},{5,4},{6,7},{7,6},{8,9},{9,8},{10,11... | collective-permute-start | bytes 9437192 | tf_op jit(solution)/shard_map/ppermute | solution.py:176
  318.8 70.8 %collective-permute-start.17 = (bf16[1024,1536]{1,0:T(8,128)(2,1)}, bf16[1024,1536]{1,0:T(8,128)(2,1)}, u32[]{:S(2)}, u32[]{:S(2)}) collective-permute-start(bf16[1024,1536]{1,0:T(8,128)(2,1)} %refs_0_.7), channel_id=1, source_target_pairs={{0,4},{1,5},{2,6},{3,7},{4,0},{5,1},{6,2},{7,3},{8,12},{9,13},{10,... | collective-permute-start | bytes 9437192 | tf_op jit(solution)/shard_map/ppermute | solution.py:176
  366.4 24.7 %collective-permute-start.21 = (bf16[1024,1536]{1,0:T(8,128)(2,1)}, bf16[1024,1536]{1,0:T(8,128)(2,1)}, u32[]{:S(2)}, u32[]{:S(2)}) collective-permute-start(bf16[1024,1536]{1,0:T(8,128)(2,1)} %get-tuple-element.112), channel_id=1, source_target_pairs={{0,1},{1,0},{2,3},{3,2},{4,5},{5,4},{6,7},{7,6},{8,9},{9,8},{10,11... | collective-permute-start | bytes 9437192 | tf_op jit(solution)/shard_map/ppermute | solution.py:176
  389.7 70.6 %collective-permute-start.15 = (bf16[1024,1536]{1,0:T(8,128)(2,1)S(1)}, bf16[1024,1536]{1,0:T(8,128)(2,1)}, u32[]{:S(2)}, u32[]{:S(2)}) collective-permute-start(bf16[1024,1536]{1,0:T(8,128)(2,1)S(1)} %copy-done.2), channel_id=1, source_target_pairs={{0,2},{1,3},{2,0},{3,1},{4,6},{5,7},{6,4},{7,5},{8,10},{9,11},{10,... | collective-permute-start | bytes 9437192 | tf_op jit(solution)/shard_map/ppermute | solution.py:176
  429.2 34.6 %collective-permute-start.22 = (bf16[1024,1536]{1,0:T(8,128)(2,1)}, bf16[1024,1536]{1,0:T(8,128)(2,1)}, u32[]{:S(2)}, u32[]{:S(2)}) collective-permute-start(bf16[1024,1536]{1,0:T(8,128)(2,1)} %get-tuple-element.117), channel_id=1, source_target_pairs={{0,1},{1,0},{2,3},{3,2},{4,5},{5,4},{6,7},{7,6},{8,9},{9,8},{10,11... | collective-permute-start | bytes 9437192 | tf_op jit(solution)/shard_map/ppermute | solution.py:176
  460.3 71.3 %collective-permute-start.5 = (bf16[1024,1536]{1,0:T(8,128)(2,1)}, bf16[1024,1536]{1,0:T(8,128)(2,1)}, u32[]{:S(2)}, u32[]{:S(2)}) collective-permute-start(bf16[1024,1536]{1,0:T(8,128)(2,1)} %get-tuple-element.90), channel_id=1, source_target_pairs={{0,2},{1,3},{2,0},{3,1},{4,6},{5,7},{6,4},{7,5},{8,10},{9,11},{10,... | collective-permute-start | bytes 9437192 | tf_op jit(solution)/shard_map/ppermute | solution.py:176
  461.8 138.0 %collective-permute-start.9 = (bf16[1024,1536]{1,0:T(8,128)(2,1)}, bf16[1024,1536]{1,0:T(8,128)(2,1)}, u32[]{:S(2)}, u32[]{:S(2)}) collective-permute-start(bf16[1024,1536]{1,0:T(8,128)(2,1)} %get-tuple-element.96), channel_id=1, source_target_pairs={{0,4},{1,5},{2,6},{3,7},{4,0},{5,1},{6,2},{7,3},{8,12},{9,13},{10,... | collective-permute-start | bytes 9437192 | tf_op jit(solution)/shard_map/ppermute | solution.py:176
  463.2 136.5 %collective-permute-start.13 = (bf16[1024,1536]{1,0:T(8,128)(2,1)}, bf16[1024,1536]{1,0:T(8,128)(2,1)}, u32[]{:S(2)}, u32[]{:S(2)}) collective-permute-start(bf16[1024,1536]{1,0:T(8,128)(2,1)} %get-tuple-element.102), channel_id=1, source_target_pairs={{0,6},{1,7},{2,4},{3,5},{4,2},{5,3},{6,0},{7,1},{8,14},{9,15},{10,... | collective-permute-start | bytes 9437192 | tf_op jit(solution)/shard_map/ppermute | solution.py:176
  502.0 110.8 %collective-permute-start.23 = (bf16[1024,1536]{1,0:T(8,128)(2,1)}, bf16[1024,1536]{1,0:T(8,128)(2,1)}, u32[]{:S(2)}, u32[]{:S(2)}) collective-permute-start(bf16[1024,1536]{1,0:T(8,128)(2,1)} %get-tuple-element.122), channel_id=1, source_target_pairs={{0,1},{1,0},{2,3},{3,2},{4,5},{5,4},{6,7},{7,6},{8,9},{9,8},{10,11... | collective-permute-start | bytes 9437192 | tf_op jit(solution)/shard_map/ppermute | solution.py:176
  502.1 129.0 %collective-permute-start.14 = (bf16[1024,1536]{1,0:T(8,128)(2,1)S(1)}, bf16[1024,1536]{1,0:T(8,128)(2,1)}, u32[]{:S(2)}, u32[]{:S(2)}) collective-permute-start(bf16[1024,1536]{1,0:T(8,128)(2,1)S(1)} %copy-done.2), channel_id=1, source_target_pairs={{0,1},{1,0},{2,3},{3,2},{4,5},{5,4},{6,7},{7,6},{8,9},{9,8},{10,11... | collective-permute-start | bytes 9437192 | tf_op jit(solution)/shard_map/ppermute | solution.py:176
  607.7 75.7 %all-to-all-start.1 = ((bf16[4,256,1536]{2,1,0:T(8,128)(2,1)}), bf16[4,256,1536]{2,1,0:T(8,128)(2,1)}, u32[]{:S(2)}, u32[]{:S(2)}) async-start(bf16[4,256,1536]{2,1,0:T(8,128)(2,1)} %bitcast.117), calls=%async_computation.1 | async-start | bytes 6291456 | tf_op jit(solution)/shard_map/all_to_all | solution.py:226
  649.2 37.7 %collective-permute-start.24 = (bf16[1024,1536]{1,0:T(8,128)(2,1)}, bf16[1024,1536]{1,0:T(8,128)(2,1)S(1)}, u32[]{:S(2)}, u32[]{:S(2)}) collective-permute-start(bf16[1024,1536]{1,0:T(8,128)(2,1)} %get-tuple-element.127), channel_id=1, source_target_pairs={{0,1},{1,0},{2,3},{3,2},{4,5},{5,4},{6,7},{7,6},{8,9},{9,8},{10,11... | collective-permute-start | bytes 9437192 | tf_op jit(solution)/shard_map/ppermute | solution.py:176
  649.3 72.3 %collective-permute-start.27 = (bf16[1024,1536]{1,0:T(8,128)(2,1)}, bf16[1024,1536]{1,0:T(8,128)(2,1)}, u32[]{:S(2)}, u32[]{:S(2)}) collective-permute-start(bf16[1024,1536]{1,0:T(8,128)(2,1)} %get-tuple-element.133), channel_id=1, source_target_pairs={{0,6},{1,7},{2,4},{3,5},{4,2},{5,3},{6,0},{7,1},{8,14},{9,15},{10,... | collective-permute-start | bytes 9437192 | tf_op jit(solution)/shard_map/ppermute | solution.py:176
  650.8 137.6 %collective-permute-start.26 = (bf16[1024,1536]{1,0:T(8,128)(2,1)}, bf16[1024,1536]{1,0:T(8,128)(2,1)}, u32[]{:S(2)}, u32[]{:S(2)}) collective-permute-start(bf16[1024,1536]{1,0:T(8,128)(2,1)} %get-tuple-element.132), channel_id=1, source_target_pairs={{0,4},{1,5},{2,6},{3,7},{4,0},{5,1},{6,2},{7,3},{8,12},{9,13},{10,... | collective-permute-start | bytes 9437192 | tf_op jit(solution)/shard_map/ppermute | solution.py:176
  652.0 136.5 %collective-permute-start.25 = (bf16[1024,1536]{1,0:T(8,128)(2,1)}, bf16[1024,1536]{1,0:T(8,128)(2,1)}, u32[]{:S(2)}, u32[]{:S(2)}) collective-permute-start(bf16[1024,1536]{1,0:T(8,128)(2,1)} %get-tuple-element.131), channel_id=1, source_target_pairs={{0,2},{1,3},{2,0},{3,1},{4,6},{5,7},{6,4},{7,5},{8,10},{9,11},{10,... | collective-permute-start | bytes 9437192 | tf_op jit(solution)/shard_map/ppermute | solution.py:176
  796.4 126.5 %all-to-all-start.2 = ((bf16[4,256,1536]{2,1,0:T(8,128)(2,1)}), bf16[4,256,1536]{2,1,0:T(8,128)(2,1)S(1)}, u32[]{:S(2)}, u32[]{:S(2)}) async-start(bf16[4,256,1536]{2,1,0:T(8,128)(2,1)} %bitcast.118), calls=%async_computation.2 | async-start | bytes 6291456 | tf_op jit(solution)/shard_map/all_to_all | solution.py:226
  801.5 280.4 %all-gather.7.cloned.1.call-start = ((), (), s32[]{:S(2)}) async-start(), calls=%async_computation.5 | async-start | bytes 3932160 | tf_op jit(solution)/shard_map/all_gather | solution.py:230
  802.2 296.3 %all-gather.11.cloned.1.call-start = ((), (), s32[]{:S(2)}) async-start(), calls=%async_computation.7 | async-start | bytes 7864320 | tf_op jit(solution)/shard_map/all_gather | solution.py:243
  924.5 174.0 %all-reduce.3.cloned.1.call-start = ((), (), s32[]{:S(2)}) async-start(), calls=%async_computation.8 | async-start | bytes 9437184 | tf_op jit(solution)/shard_map/psum | solution.py:261
  945.5 136.4 %all-to-all-start.3 = ((f32[8,8,1024]{2,1,0:T(8,128)}), f32[8,8,1024]{2,1,0:T(8,128)S(1)}, u32[]{:S(2)}, u32[]{:S(2)}) async-start(f32[8,8,1024]{2,1,0:T(8,128)} %gather_fusion.1), calls=%async_computation.3 | async-start | bytes 524288 | tf_op jit(solution)/shard_map/all_to_all | solution.py:246
  (35 other events, 369.7 us)
Sparse Core Ops, SparseCore 0:
  191.2 63.8 all-gather.4
  256.7 62.0 all-gather.8
  803.9 111.8 all-gather.6
  924.6 114.0 all-gather.10
Sparse Core Ops, SparseCore 1:
  940.5 86.4 all-reduce.2
